TPU v7x, 16 devices: a 4x2x1 block of a 4x4x8 slice. The times are simulated.
16 devices in a mesh: dp: 2 (over y, z), tp: 8 (over x, core).
Axes of the slice: x: 4, y: 2, z: 1, core: 2. Of those that a mesh axis runs over, the one named last changes fastest.
The devices are a block of a 4x4x8 slice.
Arguments:
- x_chunk: bfloat16 [8, 512, 4096], P('dp', 'tp'), parts along dimension 0
- prefix_len: int32 [8], P('dp'), parts along dimension 0
- k_cache: bfloat16 [8, 4096, 32, 128], P('dp', None, 'tp'), parts along dimension 0
- v_cache: bfloat16 [8, 4096, 32, 128], P('dp', None, 'tp'), parts along dimension 0
- ln1_gain: bfloat16 [4096], replicated
- ln1_bias: bfloat16 [4096], replicated
- w_qkv: bfloat16 [4096, 12288], P(None, 'tp')
- b_qkv: bfloat16 [12288], P('tp')
- w_out: bfloat16 [4096, 4096], P('tp')
- b_out: bfloat16 [4096], replicated
- ln2_gain: bfloat16 [4096], replicated
- ln2_bias: bfloat16 [4096], replicated
- w_up: bfloat16 [4096, 16384], P(None, 'tp')
- b_up: bfloat16 [16384], P('tp')
- w_down: bfloat16 [16384, 4096], P('tp')
- b_down: bfloat16 [4096], replicated
Outputs:
- output 1: bfloat16 [8, 512, 4096], P('dp', 'tp'), parts along dimension 0
- output 2: bfloat16 [8, 4096, 32, 128], P('dp', None, 'tp'), parts along dimension 0
- output 3: bfloat16 [8, 4096, 32, 128], P('dp', None, 'tp'), parts along dimension 0
There are 2 independent parts. A program takes and returns all parts, laid end to end along the dimension named above; an argument that names none is the same for every part.
All inputs are finite; a program needn't handle non-finite values.
Results may differ from a plain program's by a relative error of at most 0.0132093.
Values are sent between devices in bfloat16 or wider.
A program may use at most 768 MiB of HBM per device.

v0:
```python
import jax
import jax.numpy as jnp
from jax import lax
from jax.sharding import PartitionSpec as P

LN_EPS = 1e-5


def layer_norm(tok_rows, ln_gain, ln_bias):
    rows_f32 = tok_rows.astype(jnp.float32)
    row_mean = jnp.mean(rows_f32, axis=-1, keepdims=True)
    centered = rows_f32 - row_mean
    row_var = jnp.mean(centered * centered, axis=-1, keepdims=True)
    normed = centered * lax.rsqrt(row_var + LN_EPS)
    return (normed * ln_gain.astype(jnp.float32) + ln_bias.astype(jnp.float32)).astype(jnp.bfloat16)


def write_rows(cache_seq, new_rows, start_pos):
    zero_idx = jnp.zeros_like(start_pos)
    return lax.dynamic_update_slice(cache_seq, new_rows, (start_pos, zero_idx, zero_idx))


def attend(queries, k_upd, v_upd, prefix_len, head_offset, heads_all):
    batch_n, chunk_len, heads_loc, head_dim = queries.shape
    cache_len = k_upd.shape[1]
    scores = jnp.einsum('bchd,bthd->bhct', queries, k_upd, preferred_element_type=jnp.float32) * (head_dim ** -0.5)
    head_ids = head_offset + jnp.arange(heads_loc)
    slopes = jnp.exp2(-8.0 * (head_ids + 1).astype(jnp.float32) / heads_all)
    query_pos = prefix_len[:, None] + jnp.arange(chunk_len)[None, :]
    rel_pos = (jnp.arange(cache_len)[None, None, :] - query_pos[:, :, None]).astype(jnp.float32)
    scores = scores + slopes[None, :, None, None] * rel_pos[:, None]
    scores = jnp.where((rel_pos <= 0.0)[:, None], scores, -1e30)
    attn_probs = jax.nn.softmax(scores, axis=-1).astype(jnp.bfloat16)
    context = jnp.einsum('bhct,bthd->bchd', attn_probs, v_upd, preferred_element_type=jnp.float32)
    return context.astype(jnp.bfloat16).reshape(batch_n, chunk_len, heads_loc * head_dim)


def solution(mesh):
    tp_size = mesh.shape['tp']

    def local_layer(x_local, prefix_len, k_cache, v_cache, ln1_gain, ln1_bias, w_qkv, b_qkv, w_out, b_out, ln2_gain, ln2_bias, w_up, b_up, w_down, b_down):
        batch_n, tok_loc = x_local.shape[0], x_local.shape[1]
        heads_loc, head_dim = k_cache.shape[2], k_cache.shape[3]
        chunk_len = tok_loc * tp_size
        normed = layer_norm(x_local, ln1_gain, ln1_bias)
        gathered = lax.all_gather(normed, 'tp', axis=1, tiled=True)
        qkv_proj = jnp.einsum('bcd,de->bce', gathered, w_qkv, preferred_element_type=jnp.float32) + b_qkv.astype(jnp.float32)
        qkv_heads = qkv_proj.astype(jnp.bfloat16).reshape(batch_n, chunk_len, heads_loc, 3, head_dim)
        k_upd = jax.vmap(write_rows)(k_cache, qkv_heads[:, :, :, 1], prefix_len)
        v_upd = jax.vmap(write_rows)(v_cache, qkv_heads[:, :, :, 2], prefix_len)
        head_offset = lax.axis_index('tp') * heads_loc
        context = attend(qkv_heads[:, :, :, 0], k_upd, v_upd, prefix_len, head_offset, heads_loc * tp_size)
        attn_part = jnp.einsum('bce,ed->bcd', context, w_out, preferred_element_type=jnp.float32).astype(jnp.bfloat16)
        attn_sum = lax.psum_scatter(attn_part, 'tp', scatter_dimension=1, tiled=True)
        residual = (x_local.astype(jnp.float32) + attn_sum.astype(jnp.float32) + b_out.astype(jnp.float32)).astype(jnp.bfloat16)
        normed2 = layer_norm(residual, ln2_gain, ln2_bias)
        gathered2 = lax.all_gather(normed2, 'tp', axis=1, tiled=True)
        up_pre = jnp.einsum('bcd,df->bcf', gathered2, w_up, preferred_element_type=jnp.float32) + b_up.astype(jnp.float32)
        up_act = jax.nn.gelu(up_pre, approximate=True).astype(jnp.bfloat16)
        down_part = jnp.einsum('bcf,fd->bcd', up_act, w_down, preferred_element_type=jnp.float32).astype(jnp.bfloat16)
        down_sum = lax.psum_scatter(down_part, 'tp', scatter_dimension=1, tiled=True)
        x_out = (residual.astype(jnp.float32) + down_sum.astype(jnp.float32) + b_down.astype(jnp.float32)).astype(jnp.bfloat16)
        return x_out, k_upd, v_upd

    tok_spec = P('dp', 'tp', None)
    cache_spec = P('dp', None, 'tp', None)
    replicated = P()
    in_specs = (tok_spec, P('dp'), cache_spec, cache_spec, replicated, replicated, P(None, 'tp'), P('tp'), P('tp', None), replicated, replicated, replicated, P(None, 'tp'), P('tp'), P('tp', None), replicated)
    return jax.shard_map(local_layer, mesh=mesh, in_specs=in_specs, out_specs=(tok_spec, cache_spec, cache_spec), check_vma=False)
```

profile of v0, /device:TPU:112, one launch (start us, length us, event | category | flops | bytes accessed | tf_op | source)
XLA Modules:
  0.0 890.3 jit_solution(1682846422281775408)
XLA Ops:
  7.3 12.1 %copy.67 = bf16[4,4096,4,128]{3,2,1,0:T(4,128)(2,1)} copy(bf16[4,4096,4,128]{3,2,1,0:T(4,128)(2,1)} %param.18) | data formatting | bytes 33554432
  19.4 4.5 copy-done.4
  23.9 6.3 copy.68
  34.4 12.4 %broadcast_compare_fusion = pred[4,512,4096]{2,1,0:T(8,128)(4,1)} fusion(s32[4,512]{1,0:T(4,128)S(1)} %iota_add_fusion), kind=kLoop, calls=%fused_computation.38 | loop fusion | flops 25165824 | bytes 8396800 | tf_op jit(solution)/shard_map/le | solution.py:32
  46.8 11.5 %subtract_convert_fusion = f32[4,512,4096]{2,1,0:T(8,128)} fusion(s32[4,512]{1,0:T(4,128)S(1)} %iota_add_fusion), kind=kLoop, calls=%fused_computation.21 | loop fusion | flops 16777216 | bytes 33562624 | tf_op jit(solution)/shard_map/convert_element_type | solution.py:30
  58.3 59.6 %all-gather.3.cloned.1.call-done = bf16[4,512,4096]{2,1,0:T(8,128)(2,1)} async-done(((bf16[4,64,4096]{2,1,0:T(8,128)(2,1)}), bf16[4,512,4096]{2,1,0:T(8,128)(2,1)}) %all-gather.3.cloned.1.call-update) | async-done | bytes 16777232 | tf_op jit(solution)/shard_map/all_gather | solution.py:46
  117.9 33.6 %add_convert_fusion = bf16[4,512,1536]{2,1,0:T(8,128)(2,1)} fusion(f32[1536]{0:T(1024)S(1)} %convert_element_type.92, bf16[4,512,4096]{2,1,0:T(8,128)(2,1)} %all-gather.3.cloned.1.call-done, bf16[4096,1536]{1,0:T(8,128)(2,1)} %param.22), kind=kOutput, calls=%fused_computation.41 | convolution fusion | flops 25776095232 | bytes 35657728 | tf_op jit(solution)/shard_map/bcd,de->bce/dot_general | solution.py:47
  151.6 8.7 copy.27
  164.1 37.2 %while.3 = (s32[]{:T(128)}, bf16[4,4096,4,128]{3,2,1,0:T(4,128)(2,1)}, s32[4,4]{1,0:T(4,128)S(1)}, bf16[4,512,4,128]{1,3,2,0:T(8,128)(2,1)}, s32[]{:T(128)}, /*index=5*/s32[4]{0:T(128)S(1)}) while((s32[]{:T(128)}, bf16[4,4096,4,128]{3,2,1,0:T(4,128)(2,1)}, s32[4,4]{1,0:T(4,128)S(1)}, bf16[4,512,4,128]{1,3,2,0:T(8,128)(2,1)}, s32[]{:T(128)}, ...), condition=%wide.while_cond.1, body=%wide.while_body.1.sunk | while | flops 262173 | bytes 3671726 | solution.py:20
  169.5 4.0 fusion.80
  201.3 51.4 %fusion.23 = f32[4,4,512,4096]{3,2,1,0:T(8,128)} fusion(bf16[4,4096,4,128]{3,2,1,0:T(4,128)(2,1)} %get-tuple-element.16, bf16[4,512,4,3,128]{1,4,3,2,0:T(8,128)(2,1)} %bitcast.72), kind=kOutput, calls=%fused_computation.36 | convolution fusion | flops 8589934592 | bytes 153092096 | tf_op jit(solution)/shard_map/bchd,bthd->bhct/dot_general | solution.py:26
  252.8 33.2 %while.2 = (s32[]{:T(128)}, bf16[4,4096,4,128]{3,2,1,0:T(4,128)(2,1)}, s32[4,4]{1,0:T(4,128)S(1)}, bf16[4,512,4,128]{1,3,2,0:T(8,128)(2,1)S(1)}, s32[]{:T(128)}, /*index=5*/s32[4]{0:T(128)S(1)}) while((s32[]{:T(128)}, bf16[4,4096,4,128]{3,2,1,0:T(4,128)(2,1)}, s32[4,4]{1,0:T(4,128)S(1)}, bf16[4,512,4,128]{1,3,2,0:T(8,128)(2,1)S(1)}, s32[]{:T(128)}, ...), condition=%wide.while_cond, body=%wide.while_body.sunk | while | flops 262173 | bytes 3671726 | solution.py:20
  257.0 4.0 fusion.78
  265.4 4.0 fusion.78
  273.7 4.0 fusion.78
  282.0 4.0 fusion.78
  286.0 178.1 %fusion.68 = (f32[4,4,512]{2,1,0:T(4,128)S(1)}, f32[4,4,512,4096]{3,2,1,0:T(8,128)}) fusion(f32[4,4,512,4096]{3,2,1,0:T(8,128)} %fusion.23, f32[4,512,4096]{2,1,0:T(8,128)} %subtract_convert_fusion, f32[4]{0:T(128)S(1)} %multiply_exponential_fusion, pred[4,512,4096]{2,1,0:T(8,128)(4,1)} %broadcast_compare_fusion), kind=kOutput, calls=%fused_computation.94 | output fusion | flops 335548416 | bytes 310411264 | tf_op jit(solution)/shard_map/sub | solution.py:33
  464.1 48.1 %fusion.55 = bf16[4,4,128,512]{3,2,1,0:T(8,128)(2,1)S(1)} fusion(f32[4,4,512,4096]{3,2,1,0:T(8,128)} %get-tuple-element.64, f32[4,4,512]{2,1,0:T(4,128)S(1)} %get-tuple-element.63, bf16[4,4096,4,128]{3,2,1,0:T(4,128)(2,1)} %get-tuple-element.8), kind=kOutput, calls=%fused_computation.75 | convolution fusion | flops 8658092032 | bytes 153124864 | tf_op jit(solution)/shard_map/bhct,bthd->bchd/dot_general | solution.py:34
  512.2 14.6 %convolution_convert_fusion = bf16[4,512,4096]{2,1,0:T(8,128)(2,1)} fusion(bf16[4,512,512]{1,2,0:T(8,128)(2,1)S(1)} %bitcast.73, bf16[512,4096]{1,0:T(8,128)(2,1)} %param.24), kind=kOutput, calls=%fused_computation.42 | convolution fusion | flops 8598323200 | bytes 23068672 | tf_op jit(solution)/shard_map/bce,ed->bcd/dot_general | solution.py:53
  527.5 87.8 %reduce-scatter.3.cloned.1.call-done = bf16[4,64,4096]{2,1,0:T(8,128)(2,1)} async-done(((bf16[4,512,4096]{2,1,0:T(8,128)(2,1)}), bf16[4,64,4096]{2,1,0:T(8,128)(2,1)}) %reduce-scatter.3.cloned.1.call-update) | async-done | bytes 2097168 | tf_op jit(solution)/shard_map/reduce_scatter | solution.py:54
  621.9 80.6 %all-gather.5.cloned.1.call-done = bf16[4,512,4096]{2,1,0:T(8,128)(2,1)} async-done(((bf16[4,64,4096]{2,1,0:T(8,128)(2,1)}), bf16[4,512,4096]{2,1,0:T(8,128)(2,1)}) %all-gather.5.cloned.1.call-update) | async-done | bytes 16777232 | tf_op jit(solution)/shard_map/all_gather | solution.py:57
  702.5 43.0 %fusion.20 = f32[4,512,2048]{2,1,0:T(8,128)} fusion(bf16[4,512,4096]{2,1,0:T(8,128)(2,1)} %all-gather.5.cloned.1.call-done, bf16[4096,2048]{1,0:T(8,128)(2,1)} %param.28), kind=kOutput, calls=%fused_computation.33 | convolution fusion | flops 34359738368 | bytes 50331648 | tf_op jit(solution)/shard_map/bcd,df->bcf/dot_general | solution.py:58
  745.5 45.9 %fusion.27 = bf16[4,512,4096]{2,1,0:T(8,128)(2,1)} fusion(bf16[2048,4096]{1,0:T(8,128)(2,1)} %param.30, f32[4,512,2048]{2,1,0:T(8,128)} %fusion.20, f32[2048]{0:T(1024)S(1)} %convert_element_type.107), kind=kOutput, calls=%fused_computation.43 | convolution fusion | flops 34410070016 | bytes 50339840 | tf_op jit(solution)/shard_map/bcf,fd->bcd/dot_general | solution.py:60
  792.1 87.8 %reduce-scatter.5.cloned.1.call-done = bf16[4,64,4096]{2,1,0:T(8,128)(2,1)} async-done(((bf16[4,512,4096]{2,1,0:T(8,128)(2,1)}), bf16[4,64,4096]{2,1,0:T(8,128)(2,1)}) %reduce-scatter.5.cloned.1.call-update) | async-done | bytes 2097168 | tf_op jit(solution)/shard_map/reduce_scatter | solution.py:61
  (109 shorter events, 69.8 us)
Async XLA Ops:
  7.2 110.7 %all-gather.3.cloned.1.call-start = ((), (), s32[]{:S(2)}) async-start(), calls=%async_computation.2 | async-start | bytes 18874368 | tf_op jit(solution)/shard_map/all_gather | solution.py:46
  7.2 16.7 %copy-start.4 = (bf16[4,4096,4,128]{3,2,1,0:T(4,128)(2,1)S(1)}, bf16[4,4096,4,128]{3,2,1,0:T(4,128)(2,1)}, u32[]{:S(2)}) copy-start(bf16[4,4096,4,128]{3,2,1,0:T(4,128)(2,1)} %param.19) | copy-start | bytes 50331652
  23.9 6.4 copy-start.2
  23.9 7.5 copy-start.6
  23.9 7.5 copy-start.7
  23.9 10.2 %copy-start.12 = (bf16[1536]{0:T(1024)(128)(2,1)S(1)}, bf16[1536]{0:T(1024)(128)(2,1)}, u32[]{:S(2)}) copy-start(bf16[1536]{0:T(1024)(128)(2,1)} %param.23) | copy-start | bytes 9220
  23.9 10.2 %copy-start.14 = (s32[4]{0:T(128)S(1)}, s32[4]{0:T(128)}, u32[]{:S(2)}) copy-start(s32[4]{0:T(128)} %param.17) | copy-start | bytes 52
  23.9 10.2 %copy-start.15 = (s32[3]{0:T(128)S(1)}, s32[3]{0:T(128)}, u32[]{:S(2)}) copy-start(s32[3]{0:T(128)} %constant.19.clone.1) | copy-start | bytes 40
  33.8 581.5 %reduce-scatter.3.cloned.1.call-start = ((), (), s32[]{:S(2)}) async-start(), calls=%async_computation.3 | async-start | bytes 18874368 | tf_op jit(solution)/shard_map/reduce_scatter | solution.py:54
  151.6 12.6 %copy-start.5 = (s32[4]{0:T(128)S(1)}, s32[4]{0:T(128)}, u32[]{:S(2)}) copy-start(s32[4]{0:T(128)} %constant.153) | copy-start | bytes 52
  526.8 0.7 copy-start.8
  526.8 0.7 copy-start.9
  526.8 0.7 copy-start.10
  526.8 88.5 %copy-start.3 = (bf16[4,64,4096]{2,1,0:T(8,128)(2,1)S(1)}, bf16[4,64,4096]{2,1,0:T(8,128)(2,1)}, u32[]{:S(2)}) copy-start(bf16[4,64,4096]{2,1,0:T(8,128)(2,1)} %param.16) | copy-start | bytes 6291460
  526.8 95.0 %copy-start.13 = (bf16[2048]{0:T(1024)(128)(2,1)S(1)}, bf16[2048]{0:T(1024)(128)(2,1)}, u32[]{:S(2)}) copy-start(bf16[2048]{0:T(1024)(128)(2,1)} %param.29) | copy-start | bytes 12292
  526.9 175.6 %all-gather.5.cloned.1.call-start = ((), (), s32[]{:S(2)}) async-start(), calls=%async_computation.4 | async-start | bytes 18874368 | tf_op jit(solution)/shard_map/all_gather | solution.py:57
  617.9 1.3 copy-start
  621.6 258.2 %reduce-scatter.5.cloned.1.call-start = ((), (), s32[]{:S(2)}) async-start(), calls=%async_computation.5 | async-start | bytes 18874368 | tf_op jit(solution)/shard_map/reduce_scatter | solution.py:61
  791.4 0.7 copy-start.11
  791.4 88.5 %copy-start.1 = (bf16[4,64,4096]{2,1,0:T(8,128)(2,1)S(1)}, bf16[4,64,4096]{2,1,0:T(8,128)(2,1)}, u32[]{:S(2)}) copy-start(bf16[4,64,4096]{2,1,0:T(8,128)(2,1)} %copy-done) | copy-start | bytes 6291460
Sparse Core Ops, SparseCore 0:
  33.9 83.9 all-gather.2
  527.0 88.2 reduce-scatter.2
  621.7 80.7 all-gather.4
  791.6 88.2 reduce-scatter.4
where the time goes:
time: 894 us; the launch traced here: 890 us
  waiting for transfers between devices  316 us (35%)
  other arithmetic  273 us (31%)
  matrix products  237 us (27%)
  local copies, waits for them, and re-layouts  49.8 us (6%)
  between operations  14.2 us (2%)
    sub x1, other arithmetic, attend(): attn_probs = jax.nn.softmax(scores, axis=-1).astype(jnp.bfloat16)  178 us
    reduce_scatter x1, waiting for transfers between devices, local_layer(): lax.psum_scatter(down_part, 'tp', scatter_dimension=1, tiled=True)  87.8 us
    reduce_scatter x1, waiting for transfers between devices, local_layer(): lax.psum_scatter(attn_part, 'tp', scatter_dimension=1, tiled=True)  87.8 us
    all_gather x1, waiting for transfers between devices, local_layer(): gathered2 = lax.all_gather(normed2, 'tp', axis=1, tiled=True)  80.6 us
    all_gather x1, waiting for transfers between devices, local_layer(): gathered = lax.all_gather(normed, 'tp', axis=1, tiled=True)  59.6 us
    scatter x16, other arithmetic  58 us
    dot_general x1, matrix products, attend(): jnp.einsum('bchd,bthd->bhct', queries, k_upd, preferred_element_type=jnp....  51.4 us
    dot_general x1, matrix products, attend(): jnp.einsum('bhct,bthd->bchd', attn_probs, v_upd, preferred_element_type=j...  48.1 us
  transfers between devices with their start and end apart: 4, of which 4 were waited for; matrix products, arithmetic and copies ran while one was open for 3% of the time, Pallas kernels for 0%

commit v1 on v0

v1 whole, which is shorter than its diff:
```python
import functools

import jax
import jax.numpy as jnp
from jax import lax
from jax.experimental import pallas as pl
from jax.experimental.pallas import tpu as pltpu
from jax.sharding import PartitionSpec as P

LN_EPS = 1e-5
LOG2E = 1.4426950408889634
NEG = -1e30
KEY_BLOCK = 512
QUERY_SUB = 128
SPLITS = (2, 2)


def layer_norm(tok_rows, ln_gain, ln_bias):
    rows_f32 = tok_rows.astype(jnp.float32)
    row_mean = jnp.mean(rows_f32, axis=-1, keepdims=True)
    centered = rows_f32 - row_mean
    row_var = jnp.mean(centered * centered, axis=-1, keepdims=True)
    normed = centered * lax.rsqrt(row_var + LN_EPS)
    return (normed * ln_gain.astype(jnp.float32) + ln_bias.astype(jnp.float32)).astype(jnp.bfloat16)


def attend_kernel(seq0, heads, heads_all, plen_ref, head0_ref, qkv_ref, k_ref, v_ref, k_old, v_old, ctx_ref, ko_ref, vo_ref,
                  acc, row_max, row_sum, kf, vf, knew, vnew, q_t, sems):
    del k_old, v_old
    seq = pl.program_id(0)
    kb = pl.program_id(1)
    n_kb = pl.num_programs(1) - 1
    tb, hd = k_ref.shape[1] // heads, k_ref.shape[2]
    chunk = qkv_ref.shape[1]
    plen = plen_ref[seq + seq0]
    base = kb * tb
    scale = (hd ** -0.5) * LOG2E
    k_put = pltpu.make_async_copy(knew, ko_ref.at[seq + seq0, pl.ds(plen, chunk)], sems.at[0])
    v_put = pltpu.make_async_copy(vnew, vo_ref.at[seq + seq0, pl.ds(plen, chunk)], sems.at[1])

    @pl.when(kb == 0)
    def _():
        acc[...] = jnp.zeros_like(acc)
        row_max[...] = jnp.full_like(row_max, NEG)
        row_sum[...] = jnp.zeros_like(row_sum)
        for h in range(heads):
            c = h * 3 * hd
            q_t[h] = qkv_ref[0, :, c:c + hd].T
            kf[pl.ds(h, chunk, stride=heads), :] = qkv_ref[0, :, c + hd:c + 2 * hd].astype(jnp.float32)
            vf[pl.ds(h, chunk, stride=heads), :] = qkv_ref[0, :, c + 2 * hd:c + 3 * hd].astype(jnp.float32)
        knew[...] = kf[...].reshape(chunk, heads, hd).astype(jnp.bfloat16)
        vnew[...] = vf[...].reshape(chunk, heads, hd).astype(jnp.bfloat16)
        k_put.start()
        v_put.start()

    def slope(h):
        head_id = (head0_ref[0] + h + 1).astype(jnp.float32)
        return jnp.exp2(jnp.full((1, 1), -8.0 / heads_all, jnp.float32) * head_id) * LOG2E

    def step(h, keys, vals, bias_pos, mask):
        bias = slope(h) * bias_pos
        for c0 in range(0, chunk, QUERY_SUB):
            cols = slice(c0, c0 + QUERY_SUB)
            s = lax.dot_general(keys, q_t[h, :, cols], (((1,), (0,)), ((), ())), preferred_element_type=jnp.float32)
            s = s * scale + bias
            if mask is not None:
                s = jnp.where(mask if mask.shape[1] == 1 else mask[:, cols], s, NEG)
            m_old = row_max[h:h + 1, cols]
            m_new = jnp.maximum(m_old, jnp.max(s, axis=0, keepdims=True))
            alpha = jnp.exp2(m_old - m_new)
            p = jnp.exp2(s - m_new)
            row_sum[h:h + 1, cols] = row_sum[h:h + 1, cols] * alpha + jnp.sum(p, axis=0, keepdims=True)
            row_max[h:h + 1, cols] = m_new
            pv = lax.dot_general(vals, p.astype(jnp.bfloat16), (((0,), (0,)), ((), ())), preferred_element_type=jnp.float32)
            acc[h, :, cols] = acc[h, :, cols] * alpha + pv

    def prefix(masked):
        kf[...] = k_ref[0].astype(jnp.float32)
        vf[...] = v_ref[0].astype(jnp.float32)
        slot = base + lax.broadcasted_iota(jnp.int32, (tb, 1), 0)
        bias_pos = (slot - (plen + chunk - 1)).astype(jnp.float32)
        mask = (slot < plen) if masked else None
        for h in range(heads):
            keys = kf[pl.ds(h, tb, stride=heads), :].astype(jnp.bfloat16)
            vals = vf[pl.ds(h, tb, stride=heads), :].astype(jnp.bfloat16)
            step(h, keys, vals, bias_pos, mask)

    @pl.when((kb < n_kb) & (base + tb <= plen))
    def _():
        prefix(False)

    @pl.when((kb < n_kb) & (base < plen) & (base + tb > plen))
    def _():
        prefix(True)

    @pl.when(kb == n_kb)
    def _():
        key_i = lax.broadcasted_iota(jnp.int32, (chunk, chunk), 0)
        qry_i = lax.broadcasted_iota(jnp.int32, (chunk, chunk), 1)
        mask = key_i <= qry_i
        bias_pos = (lax.broadcasted_iota(jnp.int32, (chunk, 1), 0) - (chunk - 1)).astype(jnp.float32)
        for h in range(heads):
            c = h * 3 * hd
            keys = qkv_ref[0, :, c + hd:c + 2 * hd]
            vals = qkv_ref[0, :, c + 2 * hd:c + 3 * hd]
            step(h, keys, vals, bias_pos, mask)
            out = acc[h] / row_sum[h:h + 1, :]
            ctx_ref[0, :, h * hd:(h + 1) * hd] = out.T.astype(jnp.bfloat16)
        k_put.wait()
        v_put.wait()


def attend(qkv, plen, head0, k_cache, v_cache, k_out, v_out, seq0, heads_all):
    n_seq, chunk, _ = qkv.shape
    all_seq, cache_len, heads, hd = k_cache.shape
    tb = KEY_BLOCK
    n_kb = cache_len // tb

    def cache_block(b, k, plen_ref, _):
        need = (plen_ref[b + seq0] + tb - 1) // tb
        return b + seq0, jnp.minimum(k, jnp.maximum(need - 1, 0)), 0

    cache_spec = pl.BlockSpec((1, tb * heads, hd), cache_block)
    any_spec = pl.BlockSpec(memory_space=pl.ANY)
    rows = (all_seq, cache_len * heads, hd)
    grid_spec = pltpu.PrefetchScalarGridSpec(
        num_scalar_prefetch=2, grid=(n_seq, n_kb + 1),
        in_specs=[pl.BlockSpec((1, chunk, heads * 3 * hd), lambda b, k, *_: (b, 0, 0)), cache_spec, cache_spec, any_spec, any_spec],
        out_specs=[pl.BlockSpec((1, chunk, heads * hd), lambda b, k, *_: (b, 0, 0)), any_spec, any_spec],
        scratch_shapes=[pltpu.VMEM((heads, hd, chunk), jnp.float32), pltpu.VMEM((heads, chunk), jnp.float32),
                        pltpu.VMEM((heads, chunk), jnp.float32), pltpu.VMEM((tb * heads, hd), jnp.float32),
                        pltpu.VMEM((tb * heads, hd), jnp.float32), pltpu.VMEM((chunk, heads, hd), jnp.bfloat16),
                        pltpu.VMEM((chunk, heads, hd), jnp.bfloat16), pltpu.VMEM((heads, hd, chunk), jnp.bfloat16),
                        pltpu.SemaphoreType.DMA((2,))])
    return pl.pallas_call(
        functools.partial(attend_kernel, seq0, heads, heads_all), grid_spec=grid_spec,
        out_shape=[jax.ShapeDtypeStruct((n_seq, chunk, heads * hd), jnp.bfloat16),
                   jax.ShapeDtypeStruct(k_cache.shape, k_cache.dtype), jax.ShapeDtypeStruct(v_cache.shape, v_cache.dtype)],
        input_output_aliases={5: 1, 6: 2},
        cost_estimate=pl.CostEstimate(flops=4 * n_seq * heads * chunk * cache_len * hd * 3, transcendentals=0,
                                      bytes_accessed=8 * n_seq * cache_len * heads * hd),
        compiler_params=pltpu.CompilerParams(vmem_limit_bytes=60 * 1024 * 1024,
                                             dimension_semantics=("arbitrary", "arbitrary")),
    )(plen, head0, qkv, k_cache.reshape(rows), v_cache.reshape(rows), k_out, v_out)


def solution(mesh):
    tp_size = mesh.shape['tp']

    def local_layer(x_local, prefix_len, k_cache, v_cache, ln1_gain, ln1_bias, w_qkv, b_qkv, w_out, b_out, ln2_gain, ln2_bias, w_up, b_up, w_down, b_down):
        heads_loc = k_cache.shape[2]
        heads_all = heads_loc * tp_size
        head0 = (lax.axis_index('tp') * heads_loc).astype(jnp.int32).reshape(1)
        k_out, v_out = k_cache, v_cache
        bounds = [sum(SPLITS[:i]) for i in range(len(SPLITS) + 1)]
        x_parts = [x_local[lo:hi] for lo, hi in zip(bounds, bounds[1:])]
        gathered = []
        for i, x_part in enumerate(x_parts):
            if i > 0:
                x_part, normed = lax.optimization_barrier((x_part, normed))
                gathered.append(lax.all_gather(normed, 'tp', axis=1, tiled=True))
            normed = layer_norm(x_part, ln1_gain, ln1_bias)
        gathered.append(lax.all_gather(normed, 'tp', axis=1, tiled=True))
        attn_parts = []
        for i, g in enumerate(gathered):
            if i > 0:
                g, attn_parts[-1] = lax.optimization_barrier((g, attn_parts[-1]))
            qkv = (jnp.einsum('bcd,de->bce', g, w_qkv, preferred_element_type=jnp.float32) + b_qkv.astype(jnp.float32)).astype(jnp.bfloat16)
            context, k_out, v_out = attend(qkv, prefix_len, head0, k_cache, v_cache, k_out, v_out, bounds[i], heads_all)
            attn_parts.append(jnp.einsum('bce,ed->bcd', context, w_out, preferred_element_type=jnp.float32).astype(jnp.bfloat16))
        residuals, gathered2 = [], []
        for i, attn_part in enumerate(attn_parts):
            attn_sum = lax.psum_scatter(attn_part, 'tp', scatter_dimension=1, tiled=True)
            if i > 0:
                attn_sum, normed2 = lax.optimization_barrier((attn_sum, normed2))
                gathered2.append(lax.all_gather(normed2, 'tp', axis=1, tiled=True))
            residual = (x_parts[i].astype(jnp.float32) + attn_sum.astype(jnp.float32) + b_out.astype(jnp.float32)).astype(jnp.bfloat16)
            normed2 = layer_norm(residual, ln2_gain, ln2_bias)
            residuals.append(residual)
        gathered2.append(lax.all_gather(normed2, 'tp', axis=1, tiled=True))
        outs = []
        for i, g in enumerate(gathered2):
            up_pre = jnp.einsum('bcd,df->bcf', g, w_up, preferred_element_type=jnp.float32) + b_up.astype(jnp.float32)
            up_act = jax.nn.gelu(up_pre, approximate=True).astype(jnp.bfloat16)
            down_part = jnp.einsum('bcf,fd->bcd', up_act, w_down, preferred_element_type=jnp.float32).astype(jnp.bfloat16)
            down_sum = lax.psum_scatter(down_part, 'tp', scatter_dimension=1, tiled=True)
            if i > 0:
                down_sum, outs[-1] = lax.optimization_barrier((down_sum, outs[-1]))
            outs.append((residuals[i].astype(jnp.float32) + down_sum.astype(jnp.float32) + b_down.astype(jnp.float32)).astype(jnp.bfloat16))
        return jnp.concatenate(outs, axis=0), k_out, v_out

    tok_spec = P('dp', 'tp', None)
    cache_spec = P('dp', None, 'tp', None)
    replicated = P()
    in_specs = (tok_spec, P('dp'), cache_spec, cache_spec, replicated, replicated, P(None, 'tp'), P('tp'), P('tp', None), replicated, replicated, replicated, P(None, 'tp'), P('tp'), P('tp', None), replicated)
    return jax.shard_map(local_layer, mesh=mesh, in_specs=in_specs, out_specs=(tok_spec, cache_spec, cache_spec), check_vma=False)
```

time: 894 us -> 444 us (0.50)
  other arithmetic: 273 us -> 21.2 us
  waiting for transfers between devices: 316 us -> 164 us
  matrix products: 237 us -> 152 us
  Pallas kernels: 0 us -> 61.3 us
  local copies, waits for them, and re-layouts: 49.8 us -> 27.8 us
    sub x1 -> x0, other arithmetic: 178 us -> none  [attend(): attn_probs = jax.nn.softmax(scores, axis=-1).astype(jnp.bfloat16)]
    dot_general x4, matrix products: 176 us -> 81.3 us  [the longest x2 42.8 us: local_layer(): jnp.einsum('bcd,df->bcf', g, w_up, preferred_element_type=jnp.float32)]
    all_gather x2 -> x4, waiting for transfers between devices: 140 us -> 64.2 us  [the longest x2 42.5 us: local_layer(): gathered2.append(lax.all_gather(normed2, 'tp', axis=1, tiled=True))]
    pallas_call x0 -> x2, Pallas kernels: none -> 61.3 us  [attend(): pl.pallas_call(functools.partial(attend_kernel, seq0, heads, heads_all),...]
    scatter x17 -> x0, other arithmetic: 58 us -> none
    reduce_scatter x1 -> x2, waiting for transfers between devices: 87.8 us -> 47.5 us  [local_layer(): lax.psum_scatter(attn_part, 'tp', scatter_dimension=1, tiled=True)]
    reduce_scatter x1 -> x2, waiting for transfers between devices: 87.8 us -> 52.3 us  [local_layer(): lax.psum_scatter(down_part, 'tp', scatter_dimension=1, tiled=True)]
    le x1 -> x0, other arithmetic: 12.4 us -> none  [attend(): scores = jnp.where((rel_pos <= 0.0)[:, None], scores, -1e+30)]
  transfers between devices with their start and end apart: 4 -> 8, of which waited for: 4 -> 6; matrix products, arithmetic and copies ran while one was open for 3% -> 42% of each run, Pallas kernels for 0% -> 14%
where the time goes in v1:
time: 444 us; the launch traced here: 443 us
  waiting for transfers between devices  164 us (37%)
  matrix products  152 us (34%)
  Pallas kernels  61.3 us (14%)
  local copies, waits for them, and re-layouts  27.8 us (6%)
  other arithmetic  21.2 us (5%)
  between operations  14.5 us (3%)
    pallas_call x2, Pallas kernels, attend(): pl.pallas_call(functools.partial(attend_kernel, seq0, heads, heads_all),...  61.3 us
    reduce_scatter x2, waiting for transfers between devices, local_layer(): lax.psum_scatter(down_part, 'tp', scatter_dimension=1, tiled=True)  52.3 us
    dot_general x2, matrix products, local_layer(): jnp.einsum('bcf,fd->bcd', up_act, w_down, preferred_element_type=jnp.floa...  50.6 us
    reduce_scatter x2, waiting for transfers between devices, local_layer(): lax.psum_scatter(attn_part, 'tp', scatter_dimension=1, tiled=True)  47.5 us
    dot_general x2, matrix products, local_layer(): jnp.einsum('bcd,df->bcf', g, w_up, preferred_element_type=jnp.float32)  42.8 us
    all_gather x2, waiting for transfers between devices, local_layer(): gathered2.append(lax.all_gather(normed2, 'tp', axis=1, tiled=True))  42.5 us
    dot_general x2, matrix products, local_layer(): jnp.einsum('bcd,de->bce', g, w_qkv, preferred_element_type=jnp.float32)  38.5 us
    unnamed x20, local copies, waits for them, and re-layouts  26.5 us
  transfers between devices with their start and end apart: 8, of which 6 were waited for; matrix products, arithmetic and copies ran while one was open for 42% of the time, Pallas kernels for 14%

profile of v1, /device:TPU:112, one launch (start us, length us, event | category | flops | bytes accessed | tf_op | source)
XLA Modules:
  0.0 442.5 jit_solution(17781707320746913754)
XLA Ops:
  11.4 1.7 fusion.68
  13.1 2.7 fusion.71
  18.7 11.9 %copy.23.k_old = bf16[4,4096,4,128]{3,2,1,0:T(4,128)(2,1)} copy(bf16[4,4096,4,128]{3,2,1,0:T(4,128)(2,1)} %param.18) | data formatting | bytes 33554432
  30.7 11.9 %copy.24.v_old = bf16[4,4096,4,128]{3,2,1,0:T(4,128)(2,1)} copy(bf16[4,4096,4,128]{3,2,1,0:T(4,128)(2,1)} %param.19) | data formatting | bytes 33554432
  42.6 21.7 %all-gather.7.cloned.1.call-done = bf16[2,512,4096]{2,1,0:T(8,128)(2,1)} async-done(((bf16[2,64,4096]{2,1,0:T(8,128)(2,1)}), bf16[2,512,4096]{2,1,0:T(8,128)(2,1)}) %all-gather.7.cloned.1.call-update) | async-done | bytes 8388624 | tf_op jit(solution)/shard_map/all_gather | solution.py:161
  64.3 19.2 %add_convert_fusion.1.qkv_ref = bf16[2,512,1536]{2,1,0:T(8,128)(2,1)} fusion(bf16[2,512,4096]{2,1,0:T(8,128)(2,1)} %all-gather.7.cloned.1.call-done, bf16[4096,1536]{1,0:T(8,128)(2,1)} %param.22, f32[1536]{0:T(1024)S(1)} %convert_element_type.117), kind=kOutput, calls=%fused_computation.35 | convolution fusion | flops 12888047616 | bytes 24123392 | tf_op jit(solution)/shard_map/bcd,de->bce/dot_general | solution.py:168
  83.5 25.0 %shard_map.175 = (bf16[2,512,512]{2,1,0:T(8,128)(2,1)}, bf16[4,4096,4,128]{3,2,1,0:T(4,128)(2,1)}, bf16[4,4096,4,128]{3,2,1,0:T(4,128)(2,1)}) custom-call(s32[4]{0:T(128)} %plen_ref.3, s32[1]{0:T(128)} %bitcast.head0_ref, bf16[2,512,1536]{2,1,0:T(8,128)(2,1)} %add_convert_fusion.1.qkv_ref, ...), custom_call_target="tpu_custom_call", output_to_operand_aliasing={{1}: (5, {}), {2}: (6, {})} | custom-call | flops 25769803776 | bytes 33554432 | tf_op jit(solution)/shard_map/pallas_call | solution.py:135
  108.5 10.2 %convolution_convert_fusion.1 = bf16[2,512,4096]{2,1,0:T(8,128)(2,1)} fusion(bf16[2,512,512]{2,1,0:T(8,128)(2,1)} %get-tuple-element.19, bf16[512,4096]{1,0:T(8,128)(2,1)} %param.24), kind=kOutput, calls=%fused_computation.33 | convolution fusion | flops 4299161600 | bytes 13631488 | tf_op jit(solution)/shard_map/bce,ed->bcd/dot_general | solution.py:170
  118.9 19.2 %add_convert_fusion.qkv_ref = bf16[2,512,1536]{2,1,0:T(8,128)(2,1)} fusion(bf16[2,512,4096]{2,1,0:T(8,128)(2,1)} %all-gather.5.cloned.1.call-done, bf16[4096,1536]{1,0:T(8,128)(2,1)} %param.22, f32[1536]{0:T(1024)S(1)} %convert_element_type.117), kind=kOutput, calls=%fused_computation.34 | convolution fusion | flops 12888047616 | bytes 24123392 | tf_op jit(solution)/shard_map/bcd,de->bce/dot_general | solution.py:168
  138.1 36.3 %shard_map.176 = (bf16[2,512,512]{2,1,0:T(8,128)(2,1)}, bf16[4,4096,4,128]{3,2,1,0:T(4,128)(2,1)}, bf16[4,4096,4,128]{3,2,1,0:T(4,128)(2,1)}) custom-call(s32[4]{0:T(128)} %plen_ref.3, s32[1]{0:T(128)} %bitcast.head0_ref, bf16[2,512,1536]{2,1,0:T(8,128)(2,1)} %add_convert_fusion.qkv_ref, ...), custom_call_target="tpu_custom_call", output_to_operand_aliasing={{1}: (5, {}), {2}: (6, {})} | custom-call | flops 25769803776 | bytes 33554432 | tf_op jit(solution)/shard_map/pallas_call | solution.py:135
  174.5 10.2 %convolution_convert_fusion = bf16[2,512,4096]{2,1,0:T(8,128)(2,1)} fusion(bf16[2,512,512]{2,1,0:T(8,128)(2,1)} %get-tuple-element.23, bf16[512,4096]{1,0:T(8,128)(2,1)} %param.24), kind=kOutput, calls=%fused_computation.32 | convolution fusion | flops 4299161600 | bytes 13631488 | tf_op jit(solution)/shard_map/bce,ed->bcd/dot_general | solution.py:170
  186.4 1.7 convert_reduce_fusion.1
  190.0 47.4 %reduce-scatter.5.cloned.1.call-done = bf16[2,64,4096]{2,1,0:T(8,128)(2,1)} async-done(((bf16[2,512,4096]{2,1,0:T(8,128)(2,1)}), bf16[2,64,4096]{2,1,0:T(8,128)(2,1)}) %reduce-scatter.5.cloned.1.call-update) | async-done | bytes 1048592 | tf_op jit(solution)/shard_map/reduce_scatter | solution.py:173
  237.6 1.7 convert_reduce_fusion
  240.2 1.5 fusion.63
  241.9 42.1 %all-gather.11.cloned.1.call-done = bf16[2,512,4096]{2,1,0:T(8,128)(2,1)} async-done(((bf16[2,64,4096]{2,1,0:T(8,128)(2,1)}), bf16[2,512,4096]{2,1,0:T(8,128)(2,1)}) %all-gather.11.cloned.1.call-update) | async-done | bytes 8388624 | tf_op jit(solution)/shard_map/all_gather | solution.py:176
  284.0 21.3 %fusion.4 = f32[2,512,2048]{2,1,0:T(8,128)S(1)} fusion(bf16[2,512,4096]{2,1,0:T(8,128)(2,1)} %all-gather.11.cloned.1.call-done, bf16[4096,2048]{1,0:T(8,128)(2,1)} %param.28), kind=kOutput, calls=%fused_computation.4 | convolution fusion | flops 17179869184 | bytes 33554432 | tf_op jit(solution)/shard_map/bcd,df->bcf/dot_general | solution.py:183
  305.3 25.3 %fusion.31 = bf16[2,512,4096]{2,1,0:T(8,128)(2,1)} fusion(bf16[2048,4096]{1,0:T(8,128)(2,1)} %param.30, f32[2,512,2048]{2,1,0:T(8,128)S(1)} %fusion.4, f32[2048]{0:T(1024)S(1)} %convert_element_type.133), kind=kOutput, calls=%fused_computation.31 | convolution fusion | flops 17205035008 | bytes 33562624 | tf_op jit(solution)/shard_map/bcf,fd->bcd/dot_general | solution.py:185
  331.1 21.5 %fusion.6 = f32[2,512,2048]{2,1,0:T(8,128)S(1)} fusion(bf16[2,512,4096]{2,1,0:T(8,128)(2,1)} %all-gather.9.cloned.1.call-done, bf16[4096,2048]{1,0:T(8,128)(2,1)} %param.28), kind=kOutput, calls=%fused_computation.6 | convolution fusion | flops 17179869184 | bytes 33554432 | tf_op jit(solution)/shard_map/bcd,df->bcf/dot_general | solution.py:183
  352.6 25.3 %fusion.28 = bf16[2,512,4096]{2,1,0:T(8,128)(2,1)} fusion(bf16[2048,4096]{1,0:T(8,128)(2,1)} %param.30, f32[2,512,2048]{2,1,0:T(8,128)S(1)} %fusion.6, f32[2048]{0:T(1024)S(1)} %convert_element_type.133), kind=kOutput, calls=%fused_computation.30 | convolution fusion | flops 17205035008 | bytes 33562624 | tf_op jit(solution)/shard_map/bcf,fd->bcd/dot_general | solution.py:185
  378.6 3.5 reduce-scatter.11.cloned.1.call-done
  382.1 1.5 fusion.79
  383.6 48.8 %reduce-scatter.9.cloned.1.call-done = bf16[2,64,4096]{2,1,0:T(8,128)(2,1)} async-done(((bf16[2,512,4096]{2,1,0:T(8,128)(2,1)}), bf16[2,64,4096]{2,1,0:T(8,128)(2,1)}) %reduce-scatter.9.cloned.1.call-update) | async-done | bytes 1048592 | tf_op jit(solution)/shard_map/reduce_scatter | solution.py:186
  432.5 1.5 fusion.81
  (62 shorter events, 14.7 us)
Async XLA Ops:
  7.2 11.5 %copy-start.7 = (bf16[1536]{0:T(1024)(128)(2,1)S(1)}, bf16[1536]{0:T(1024)(128)(2,1)}, u32[]{:S(2)}) copy-start(bf16[1536]{0:T(1024)(128)(2,1)} %param.23) | copy-start | bytes 9220
  7.2 57.1 %all-gather.7.cloned.1.call-start = ((), (), s32[]{:S(2)}) async-start(), calls=%async_computation.5 | async-start | bytes 9437184 | tf_op jit(solution)/shard_map/all_gather | solution.py:161
  15.8 102.9 %all-gather.5.cloned.1.call-start = ((), (), s32[]{:S(2)}) async-start(), calls=%async_computation.4 | async-start | bytes 9437184 | tf_op jit(solution)/shard_map/all_gather | solution.py:163
  18.1 167.4 %reduce-scatter.7.cloned.1.call-start = ((), (), s32[]{:S(2)}) async-start(), calls=%async_computation.7 | async-start | bytes 9437184 | tf_op jit(solution)/shard_map/reduce_scatter | solution.py:173
  118.8 118.6 %reduce-scatter.5.cloned.1.call-start = ((), (), s32[]{:S(2)}) async-start(), calls=%async_computation.6 | async-start | bytes 9437184 | tf_op jit(solution)/shard_map/reduce_scatter | solution.py:173
  184.7 0.7 copy-start.3
  184.7 0.7 copy-start.4
  184.7 0.7 copy-start.5
  184.7 1.6 copy-start
  184.8 99.2 %all-gather.11.cloned.1.call-start = ((), (), s32[]{:S(2)}) async-start(), calls=%async_computation.10 | async-start | bytes 9437184 | tf_op jit(solution)/shard_map/all_gather | solution.py:176
  188.0 53.8 %copy-start.8 = (bf16[2048]{0:T(1024)(128)(2,1)S(1)}, bf16[2048]{0:T(1024)(128)(2,1)}, u32[]{:S(2)}) copy-start(bf16[2048]{0:T(1024)(128)(2,1)} %param.29) | copy-start | bytes 12292
  237.5 93.6 %all-gather.9.cloned.1.call-start = ((), (), s32[]{:S(2)}) async-start(), calls=%async_computation.8 | async-start | bytes 9437184 | tf_op jit(solution)/shard_map/all_gather | solution.py:180
  239.2 1.0 copy-start.1
  241.8 140.3 %reduce-scatter.11.cloned.1.call-start = ((), (), s32[]{:S(2)}) async-start(), calls=%async_computation.11 | async-start | bytes 9437184 | tf_op jit(solution)/shard_map/reduce_scatter | solution.py:186
  330.6 101.8 %reduce-scatter.9.cloned.1.call-start = ((), (), s32[]{:S(2)}) async-start(), calls=%async_computation.9 | async-start | bytes 9437184 | tf_op jit(solution)/shard_map/reduce_scatter | solution.py:186
  377.9 0.7 copy-start.6
  377.9 54.5 %copy-start.2 = (bf16[2,64,4096]{2,1,0:T(8,128)(2,1)S(1)}, bf16[2,64,4096]{2,1,0:T(8,128)(2,1)}, u32[]{:S(2)}) copy-start(bf16[2,64,4096]{2,1,0:T(8,128)(2,1)} %copy-done.1) | copy-start | bytes 3145732
Sparse Core Ops, SparseCore 0:
  15.9 48.2 all-gather.6
  66.4 45.6 all-gather.4
  118.9 54.4 reduce-scatter.6
  184.9 52.4 reduce-scatter.4
  238.9 45.0 all-gather.10
  285.4 45.6 all-gather.8
  333.4 48.6 reduce-scatter.10
  384.4 48.0 reduce-scatter.8

commit v2 on v1

--- a/solution.py
+++ b/solution.py
@@ -144,6 +144,23 @@
     )(plen, head0, qkv, k_cache.reshape(rows), v_cache.reshape(rows), k_out, v_out)
 
 
+def copy_kernel(src_ref, dst_ref):
+    dst_ref[...] = src_ref[...]
+
+
+def copy_cache(cache):
+    seqs, cache_len, heads, hd = cache.shape
+    rows = cache_len * heads
+    spec = pl.BlockSpec((1, rows // 4, hd), lambda b, k: (b, k, 0))
+    out = pl.pallas_call(
+        copy_kernel, grid=(seqs, 4), in_specs=[spec], out_specs=spec,
+        out_shape=jax.ShapeDtypeStruct((seqs, rows, hd), cache.dtype),
+        cost_estimate=pl.CostEstimate(flops=seqs * rows * hd * 1000, transcendentals=0, bytes_accessed=4 * seqs * rows * hd),
+        compiler_params=pltpu.CompilerParams(vmem_limit_bytes=60 * 1024 * 1024),
+    )(cache.reshape(seqs, rows, hd))
+    return out.reshape(cache.shape)
+
+
 def solution(mesh):
     tp_size = mesh.shape['tp']
 
@@ -151,43 +168,77 @@
         heads_loc = k_cache.shape[2]
         heads_all = heads_loc * tp_size
         head0 = (lax.axis_index('tp') * heads_loc).astype(jnp.int32).reshape(1)
-        k_out, v_out = k_cache, v_cache
-        bounds = [sum(SPLITS[:i]) for i in range(len(SPLITS) + 1)]
-        x_parts = [x_local[lo:hi] for lo, hi in zip(bounds, bounds[1:])]
-        gathered = []
-        for i, x_part in enumerate(x_parts):
-            if i > 0:
-                x_part, normed = lax.optimization_barrier((x_part, normed))
-                gathered.append(lax.all_gather(normed, 'tp', axis=1, tiled=True))
-            normed = layer_norm(x_part, ln1_gain, ln1_bias)
-        gathered.append(lax.all_gather(normed, 'tp', axis=1, tiled=True))
-        attn_parts = []
-        for i, g in enumerate(gathered):
-            if i > 0:
-                g, attn_parts[-1] = lax.optimization_barrier((g, attn_parts[-1]))
-            qkv = (jnp.einsum('bcd,de->bce', g, w_qkv, preferred_element_type=jnp.float32) + b_qkv.astype(jnp.float32)).astype(jnp.bfloat16)
-            context, k_out, v_out = attend(qkv, prefix_len, head0, k_cache, v_cache, k_out, v_out, bounds[i], heads_all)
-            attn_parts.append(jnp.einsum('bce,ed->bcd', context, w_out, preferred_element_type=jnp.float32).astype(jnp.bfloat16))
-        residuals, gathered2 = [], []
-        for i, attn_part in enumerate(attn_parts):
-            attn_sum = lax.psum_scatter(attn_part, 'tp', scatter_dimension=1, tiled=True)
-            if i > 0:
-                attn_sum, normed2 = lax.optimization_barrier((attn_sum, normed2))
-                gathered2.append(lax.all_gather(normed2, 'tp', axis=1, tiled=True))
-            residual = (x_parts[i].astype(jnp.float32) + attn_sum.astype(jnp.float32) + b_out.astype(jnp.float32)).astype(jnp.bfloat16)
-            normed2 = layer_norm(residual, ln2_gain, ln2_bias)
-            residuals.append(residual)
-        gathered2.append(lax.all_gather(normed2, 'tp', axis=1, tiled=True))
-        outs = []
-        for i, g in enumerate(gathered2):
-            up_pre = jnp.einsum('bcd,df->bcf', g, w_up, preferred_element_type=jnp.float32) + b_up.astype(jnp.float32)
-            up_act = jax.nn.gelu(up_pre, approximate=True).astype(jnp.bfloat16)
-            down_part = jnp.einsum('bcf,fd->bcd', up_act, w_down, preferred_element_type=jnp.float32).astype(jnp.bfloat16)
-            down_sum = lax.psum_scatter(down_part, 'tp', scatter_dimension=1, tiled=True)
-            if i > 0:
-                down_sum, outs[-1] = lax.optimization_barrier((down_sum, outs[-1]))
-            outs.append((residuals[i].astype(jnp.float32) + down_sum.astype(jnp.float32) + b_down.astype(jnp.float32)).astype(jnp.bfloat16))
-        return jnp.concatenate(outs, axis=0), k_out, v_out
+        core = lax.rem(lax.axis_index('tp'), 2)
+        chips = tp_size // 2
+        groups = [[chip * 2 + c for chip in range(chips)] for c in range(2)]
+        swap = [(i, i ^ 1) for i in range(tp_size)]
+        barrier = lax.optimization_barrier
+        half = SPLITS[0]
+        x_parts = [x_local[None, :half], x_local[None, half:]]
+
+        def gather(rows):
+            return lax.all_gather(rows, 'tp', axis=0, tiled=True, axis_index_groups=groups)
+
+        def scatter(rows):
+            return lax.psum_scatter(rows, 'tp', scatter_dimension=0, tiled=True, axis_index_groups=groups)
+
+        def to_partner(rows):
+            return lax.ppermute(rows, 'tp', swap)
+
+        def matmul(rows, weight):
+            return jnp.einsum('xbtc,cd->xbtd', rows, weight, preferred_element_type=jnp.float32)
+
+        def chip_sum(for_partner, own, weight):
+            received = to_partner(matmul(for_partner, weight).astype(jnp.bfloat16))
+            return (matmul(own, weight) + received.astype(jnp.float32)).astype(jnp.bfloat16)
+
+        def project_qkv(g):
+            own, partner = [(matmul(rows, w_qkv) + b_qkv.astype(jnp.float32)).astype(jnp.bfloat16) for rows in (g, to_partner(g))]
+            first = core == 0
+            pair = jnp.stack([jnp.where(first, own, partner), jnp.where(first, partner, own)], axis=1)
+            return jnp.transpose(pair, (2, 0, 1, 3, 4)).reshape(own.shape[1], -1, own.shape[-1])
+
+        def project_out(context):
+            pairs = context.reshape(context.shape[0], chips, 2, x_local.shape[1], context.shape[-1])
+            own = lax.dynamic_index_in_dim(pairs, core, axis=2, keepdims=False)
+            partner = lax.dynamic_index_in_dim(pairs, 1 - core, axis=2, keepdims=False)
+            return chip_sum(jnp.swapaxes(partner, 0, 1), jnp.swapaxes(own, 0, 1), w_out)
+
+        def add_bias(rows, total, bias):
+            return (rows.astype(jnp.float32) + total.astype(jnp.float32) + bias.astype(jnp.float32)).astype(jnp.bfloat16)
+
+        def mlp(g):
+            own, partner = [
+                jax.nn.gelu(matmul(rows, w_up) + b_up.astype(jnp.float32), approximate=True).astype(jnp.bfloat16)
+                for rows in (g, to_partner(g))]
+            return chip_sum(partner, own, w_down)
+
+        norm_a = layer_norm(x_parts[0], ln1_gain, ln1_bias)
+        x_b, norm_a = barrier((x_parts[1], norm_a))
+        gath_a = gather(norm_a)
+        gath_b = gather(layer_norm(x_b, ln1_gain, ln1_bias))
+        k_out, v_out = copy_cache(k_cache), copy_cache(v_cache)
+        gath_a, k_out, v_out = barrier((gath_a, k_out, v_out))
+        ctx_a, k_out, v_out = attend(project_qkv(gath_a), prefix_len, head0, k_cache, v_cache, k_out, v_out, 0, heads_all)
+        part_a = project_out(ctx_a)
+        gath_b, part_a = barrier((gath_b, part_a))
+        sum_a = scatter(part_a)
+        ctx_b, k_out, v_out = attend(project_qkv(gath_b), prefix_len, head0, k_cache, v_cache, k_out, v_out, half, heads_all)
+        res_a = add_bias(x_parts[0], sum_a, b_out)
+        norm_a = layer_norm(res_a, ln2_gain, ln2_bias)
+        ctx_b, norm_a = barrier((ctx_b, norm_a))
+        gath_a = gather(norm_a)
+        sum_b = scatter(project_out(ctx_b))
+        down_a = mlp(gath_a)
+        res_b = add_bias(x_parts[1], sum_b, b_out)
+        gath_b = gather(layer_norm(res_b, ln2_gain, ln2_bias))
+        gath_b, down_a = barrier((gath_b, down_a))
+        tot_a = scatter(down_a)
+        tot_b = scatter(mlp(gath_b))
+        out_a = add_bias(res_a, tot_a, b_down)
+        tot_b, out_a = barrier((tot_b, out_a))
+        out_b = add_bias(res_b, tot_b, b_down)
+        return jnp.concatenate([out_a, out_b], axis=1)[0], k_out, v_out
 
     tok_spec = P('dp', 'tp', None)
     cache_spec = P('dp', None, 'tp', None)

time: 444 us -> 486 us (1.095)
  matrix products: 152 us -> 194 us
  Pallas kernels: 61.3 us -> 90.8 us
  local copies, waits for them, and re-layouts: 27.8 us -> 9.78 us
  waiting for transfers between devices: 164 us -> 147 us
    reduce_scatter x4, waiting for transfers between devices: 99.8 us -> 58.1 us  [scatter(): lax.psum_scatter(rows, 'tp', scatter_dimension=0, tiled=True, axis_index_...]
    dot_general x8 -> x12, matrix products: 152 us -> 194 us  [matmul(): jnp.einsum('xbtc,cd->xbtd', rows, weight, preferred_element_type=jnp.floa...]
    pallas_call x0 -> x2, Pallas kernels: none -> 34.9 us  [copy_cache(): pl.pallas_call(copy_kernel, grid=(seqs, 4), in_specs=[spec], out_specs=sp...]
    unnamed x20 -> x28, local copies, waits for them, and re-layouts: 26.5 us -> 2.39 us
    ppermute x0 -> x8, waiting for transfers between devices: none -> 20.7 us  [to_partner(): return lax.ppermute(rows, 'tp', swap)]
    pallas_call x2, Pallas kernels: 61.3 us -> 55.9 us  [attend(): pl.pallas_call(functools.partial(attend_kernel, seq0, heads, heads_all),...]
  transfers between devices with their start and end apart: 8 -> 16, of which waited for: 6 -> 9; matrix products, arithmetic and copies ran while one was open for 42% -> 37% of each run, Pallas kernels for 14% -> 19%
where the time goes in v2:
time: 486 us; the launch traced here: 480 us
  matrix products  194 us (40%)
  waiting for transfers between devices  147 us (30%)
  Pallas kernels  90.8 us (19%)
  other arithmetic  20.7 us (4%)
  between operations  14.9 us (3%)
  local copies, waits for them, and re-layouts  9.78 us (2%)
    dot_general x12, matrix products, matmul(): jnp.einsum('xbtc,cd->xbtd', rows, weight, preferred_element_type=jnp.floa...  194 us
    all_gather x4, waiting for transfers between devices, gather(): lax.all_gather(rows, 'tp', axis=0, tiled=True, axis_index_groups=groups)  67.9 us
    reduce_scatter x4, waiting for transfers between devices, scatter(): lax.psum_scatter(rows, 'tp', scatter_dimension=0, tiled=True, axis_index_...  58.1 us
    pallas_call x2, Pallas kernels, attend(): pl.pallas_call(functools.partial(attend_kernel, seq0, heads, heads_all),...  55.9 us
    pallas_call x2, Pallas kernels, copy_cache(): pl.pallas_call(copy_kernel, grid=(seqs, 4), in_specs=[spec], out_specs=sp...  34.9 us
    ppermute x8, waiting for transfers between devices, to_partner(): return lax.ppermute(rows, 'tp', swap)  20.7 us
  transfers between devices with their start and end apart: 16, of which 9 were waited for; matrix products, arithmetic and copies ran while one was open for 37% of the time, Pallas kernels for 19%

profile of v2, /device:TPU:112, one launch (start us, length us, event | category | flops | bytes accessed | tf_op | source)
XLA Modules:
  0.0 480.1 jit_solution(8277126158402801)
XLA Ops:
  14.8 17.4 %shard_map.175 = bf16[4,16384,128]{2,1,0:T(8,128)(2,1)} custom-call(bf16[4,16384,128]{2,1,0:T(8,128)(2,1)} %bitcast.163), custom_call_target="tpu_custom_call" | custom-call | flops 8388608000 | bytes 33554432 | tf_op jit(solution)/shard_map/pallas_call | solution.py:155
  32.2 17.4 %shard_map.176 = bf16[4,16384,128]{2,1,0:T(8,128)(2,1)} custom-call(bf16[4,16384,128]{2,1,0:T(8,128)(2,1)} %bitcast.166), custom_call_target="tpu_custom_call" | custom-call | flops 8388608000 | bytes 33554432 | tf_op jit(solution)/shard_map/pallas_call | solution.py:155
  49.7 12.1 %all-gather.7.cloned.1.call-done = bf16[4,2,64,4096]{3,2,1,0:T(8,128)(2,1)} async-done(((bf16[1,2,64,4096]{3,2,1,0:T(8,128)(2,1)}), bf16[4,2,64,4096]{3,2,1,0:T(8,128)(2,1)}) %all-gather.7.cloned.1.call-update) | async-done | bytes 4194320 | tf_op jit(solution)/shard_map/all_gather | solution.py:180
  64.0 10.9 %fusion.117 = bf16[4,2,64,1536]{3,2,1,0:T(8,128)(2,1)S(1)} fusion(bf16[4,2,64,4096]{3,2,1,0:T(8,128)(2,1)} %all-gather.7.cloned.1.call-done, bf16[4096,1536]{1,0:T(8,128)(2,1)} %param.22, f32[1536]{0:T(1024)S(1)} %convert_element_type.168), kind=kOutput, calls=%fused_computation.92 | convolution fusion | flops 6444023808 | bytes 18356224 | tf_op jit(solution)/shard_map/xbtc,cd->xbtd/dot_general | solution.py:189
  75.0 10.9 %select_bitcast_fusion.3 = (bf16[4,1,2,64,1536]{4,3,2,0,1:T(8,128)(2,1)S(1)}, bf16[4,1,2,64,1536]{4,3,2,0,1:T(8,128)(2,1)S(1)}) fusion(bf16[4,2,64,1536]{3,2,1,0:T(8,128)(2,1)S(1)} %fusion.117, pred[]{:T(512)S(6)} %eq.4, f32[1536]{0:T(1024)S(1)} %convert_element_type.168, bf16[4,2,64,4096]{3,2,1,0:T(8,128)(2,1)} %collective-permute-done, ...), kind=kOutput, calls=%fused_computation.151 | convolution fusion | flops 6445596672 | bytes 21501952 | tf_op jit(solution)/shard_map/xbtc,cd->xbtd/dot_general | solution.py:189
  88.1 30.6 %shard_map.177 = (bf16[2,512,512]{2,1,0:T(8,128)(2,1)}, bf16[4,4096,4,128]{3,2,1,0:T(4,128)(2,1)}, bf16[4,4096,4,128]{3,2,1,0:T(4,128)(2,1)}) custom-call(s32[4]{0:T(128)} %plen_ref.3, s32[1]{0:T(128)} %bitcast.1.head0_ref, bf16[2,512,1536]{2,1,0:T(8,128)(2,1)} %bitcast.172, ...), custom_call_target="tpu_custom_call", output_to_operand_aliasing={{1}: (5, {}), {2}: (6, {})} | custom-call | flops 25769803776 | bytes 33554432 | tf_op jit(solution)/shard_map/pallas_call | solution.py:135
  120.0 4.7 convolution_convert_fusion.1
  125.3 6.8 %collective-permute-done.1 = bf16[4,2,64,4096]{3,2,1,0:T(8,128)(2,1)S(1)} collective-permute-done((bf16[4,2,64,4096]{3,2,1,0:T(8,128)(2,1)S(1)}, bf16[4,2,64,4096]{3,2,1,0:T(8,128)(2,1)S(1)}, u32[]{:S(2)}, u32[]{:S(2)}) %collective-permute-start.1) | collective-permute-done | bytes 4194336 | tf_op jit(solution)/shard_map/ppermute | solution.py:186
  132.1 4.3 add_convert_fusion.3
  137.1 11.2 %fusion.111 = bf16[4,2,64,1536]{3,2,1,0:T(8,128)(2,1)S(1)} fusion(bf16[4,2,64,4096]{3,2,1,0:T(8,128)(2,1)} %all-gather.5.cloned.1.call-done, bf16[4096,1536]{1,0:T(8,128)(2,1)} %param.22, f32[1536]{0:T(1024)S(1)} %convert_element_type.168), kind=kOutput, calls=%fused_computation.90 | convolution fusion | flops 6444023808 | bytes 18356224 | tf_op jit(solution)/shard_map/xbtc,cd->xbtd/dot_general | solution.py:189
  148.3 10.9 %select_bitcast_fusion.1 = (bf16[4,1,2,64,1536]{4,3,2,0,1:T(8,128)(2,1)S(1)}, bf16[4,1,2,64,1536]{4,3,2,0,1:T(8,128)(2,1)S(1)}) fusion(bf16[4,2,64,1536]{3,2,1,0:T(8,128)(2,1)S(1)} %fusion.111, pred[]{:T(512)S(6)} %eq.4, f32[1536]{0:T(1024)S(1)} %convert_element_type.168, bf16[4,2,64,4096]{3,2,1,0:T(8,128)(2,1)} %collective-permute-done.2, ...), kind=kOutput, calls=%fused_computation.149 | convolution fusion | flops 6445596672 | bytes 21501952 | tf_op jit(solution)/shard_map/xbtc,cd->xbtd/dot_general | solution.py:189
  161.4 25.4 %shard_map.178 = (bf16[2,512,512]{2,1,0:T(8,128)(2,1)}, bf16[4,4096,4,128]{3,2,1,0:T(4,128)(2,1)}, bf16[4,4096,4,128]{3,2,1,0:T(4,128)(2,1)}) custom-call(s32[4]{0:T(128)} %plen_ref.3, s32[1]{0:T(128)} %bitcast.1.head0_ref, bf16[2,512,1536]{2,1,0:T(8,128)(2,1)} %bitcast.171, ...), custom_call_target="tpu_custom_call", output_to_operand_aliasing={{1}: (5, {}), {2}: (6, {})} | custom-call | flops 25769803776 | bytes 33554432 | tf_op jit(solution)/shard_map/pallas_call | solution.py:135
  192.3 6.6 %convolution_convert_fusion = bf16[4,2,64,4096]{3,2,1,0:T(8,128)(2,1)} fusion(bf16[512,4096]{1,0:T(8,128)(2,1)} %param.24, bf16[2,4,1,64,512]{4,3,2,1,0:T(8,128)(2,1)S(1)} %get-tuple-element.50), kind=kOutput, calls=%fused_computation.32 | convolution fusion | flops 2149580800 | bytes 8912896 | tf_op jit(solution)/shard_map/xbtc,cd->xbtd/dot_general | solution.py:189
  199.3 44.2 %all-gather.11.cloned.1.call-done = bf16[4,2,64,4096]{3,2,1,0:T(8,128)(2,1)} async-done(((bf16[1,2,64,4096]{3,2,1,0:T(8,128)(2,1)}), bf16[4,2,64,4096]{3,2,1,0:T(8,128)(2,1)}) %all-gather.11.cloned.1.call-update) | async-done | bytes 4194320 | tf_op jit(solution)/shard_map/all_gather | solution.py:180
  243.5 7.8 %add_convert_fusion.2 = bf16[4,2,64,4096]{3,2,1,0:T(8,128)(2,1)} fusion(bf16[4,2,64,4096]{3,2,1,0:T(8,128)(2,1)} %collective-permute-done.3, bf16[512,4096]{1,0:T(8,128)(2,1)} %param.24, bf16[2,4,1,64,512]{4,3,2,1,0:T(8,128)(2,1)S(1)} %copy-done.6), kind=kOutput, calls=%fused_computation.26 | convolution fusion | flops 2153775104 | bytes 13107200 | tf_op jit(solution)/shard_map/xbtc,cd->xbtd/dot_general | solution.py:189
  251.9 31.2 %fusion.24 = bf16[4,2,64,4096]{3,2,1,0:T(8,128)(2,1)} fusion(bf16[2048,4096]{1,0:T(8,128)(2,1)} %param.30, bf16[4,2,64,4096]{3,2,1,0:T(8,128)(2,1)} %collective-permute-done.4, bf16[4096,2048]{1,0:T(8,128)(2,1)} %param.28, f32[2048]{0:T(1024)S(1)} %convert_element_type.191), kind=kOutput, calls=%fused_computation.34 | convolution fusion | flops 17192452096 | bytes 41951232 | tf_op jit(solution)/shard_map/xbtc,cd->xbtd/dot_general | solution.py:189
  283.7 11.1 %reduce-scatter.7.cloned.1.call-done = bf16[1,2,64,4096]{3,2,1,0:T(8,128)(2,1)} async-done(((bf16[4,2,64,4096]{3,2,1,0:T(8,128)(2,1)}), bf16[1,2,64,4096]{3,2,1,0:T(8,128)(2,1)}) %reduce-scatter.7.cloned.1.call-update) | async-done | bytes 1048592 | tf_op jit(solution)/shard_map/reduce_scatter | solution.py:183
  299.3 31.9 %add_convert_fusion.1 = bf16[4,2,64,4096]{3,2,1,0:T(8,128)(2,1)} fusion(bf16[4,2,64,4096]{3,2,1,0:T(8,128)(2,1)} %collective-permute-done.5, bf16[2048,4096]{1,0:T(8,128)(2,1)} %param.30, bf16[4,2,64,4096]{3,2,1,0:T(8,128)(2,1)} %all-gather.11.cloned.1.call-done, bf16[4096,2048]{1,0:T(8,128)(2,1)} %param.28, f32[2048]{0:T(1024)S(1)} %convert_element_type.191), kind=kOutput, calls=%fused_computation.25 | convolution fusion | flops 17196646400 | bytes 46145536 | tf_op jit(solution)/shard_map/xbtc,cd->xbtd/dot_general | solution.py:189
  331.1 11.7 %all-gather.9.cloned.1.call-done = bf16[4,2,64,4096]{3,2,1,0:T(8,128)(2,1)} async-done(((bf16[1,2,64,4096]{3,2,1,0:T(8,128)(2,1)}), bf16[4,2,64,4096]{3,2,1,0:T(8,128)(2,1)}) %all-gather.9.cloned.1.call-update) | async-done | bytes 4194320 | tf_op jit(solution)/shard_map/all_gather | solution.py:180
  342.8 7.1 %collective-permute-done.6 = bf16[4,2,64,4096]{3,2,1,0:T(8,128)(2,1)} collective-permute-done((bf16[4,2,64,4096]{3,2,1,0:T(8,128)(2,1)}, bf16[4,2,64,4096]{3,2,1,0:T(8,128)(2,1)}, u32[]{:S(2)}, u32[]{:S(2)}) %collective-permute-start.6) | collective-permute-done | bytes 4194336 | tf_op jit(solution)/shard_map/ppermute | solution.py:186
  349.9 31.4 %fusion.27 = bf16[4,2,64,4096]{3,2,1,0:T(8,128)(2,1)} fusion(bf16[2048,4096]{1,0:T(8,128)(2,1)} %param.30, bf16[4,2,64,4096]{3,2,1,0:T(8,128)(2,1)} %collective-permute-done.6, bf16[4096,2048]{1,0:T(8,128)(2,1)} %param.28, f32[2048]{0:T(1024)S(1)} %convert_element_type.191), kind=kOutput, calls=%fused_computation.35 | convolution fusion | flops 17192452096 | bytes 41951232 | tf_op jit(solution)/shard_map/xbtc,cd->xbtd/dot_general | solution.py:189
  381.6 6.8 %collective-permute-done.7 = bf16[4,2,64,4096]{3,2,1,0:T(8,128)(2,1)} collective-permute-done((bf16[4,2,64,4096]{3,2,1,0:T(8,128)(2,1)}, bf16[4,2,64,4096]{3,2,1,0:T(8,128)(2,1)}, u32[]{:S(2)}, u32[]{:S(2)}) %collective-permute-start.7) | collective-permute-done | bytes 4194336 | tf_op jit(solution)/shard_map/ppermute | solution.py:186
  388.4 32.1 %add_convert_fusion = bf16[4,2,64,4096]{3,2,1,0:T(8,128)(2,1)} fusion(bf16[4,2,64,4096]{3,2,1,0:T(8,128)(2,1)} %collective-permute-done.7, bf16[2048,4096]{1,0:T(8,128)(2,1)} %param.30, bf16[4,2,64,4096]{3,2,1,0:T(8,128)(2,1)} %all-gather.9.cloned.1.call-done, bf16[4096,2048]{1,0:T(8,128)(2,1)} %param.28, f32[2048]{0:T(1024)S(1)} %convert_element_type.191), kind=kOutput, calls=%fused_computation.24 | convolution fusion | flops 17196646400 | bytes 46145536 | tf_op jit(solution)/shard_map/xbtc,cd->xbtd/dot_general | solution.py:189
  426.4 43.2 %reduce-scatter.9.cloned.1.call-done = bf16[1,2,64,4096]{3,2,1,0:T(8,128)(2,1)} async-done(((bf16[4,2,64,4096]{3,2,1,0:T(8,128)(2,1)}), bf16[1,2,64,4096]{3,2,1,0:T(8,128)(2,1)}) %reduce-scatter.9.cloned.1.call-update) | async-done | bytes 1048592 | tf_op jit(solution)/shard_map/reduce_scatter | solution.py:183
  (98 shorter events, 37.7 us)
Async XLA Ops:
  7.2 6.0 %copy-start = (bf16[4,64,4096]{2,1,0:T(8,128)(2,1)S(1)}, bf16[4,64,4096]{2,1,0:T(8,128)(2,1)}, u32[]{:S(2)}) copy-start(bf16[4,64,4096]{2,1,0:T(8,128)(2,1)} %param.16) | copy-start | bytes 6291460
  7.2 54.5 %all-gather.7.cloned.1.call-start = ((), (), s32[]{:S(2)}) async-start(), calls=%async_computation.5 | async-start | bytes 5242880 | tf_op jit(solution)/shard_map/all_gather | solution.py:180
  14.7 121.7 %all-gather.5.cloned.1.call-start = ((), (), s32[]{:S(2)}) async-start(), calls=%async_computation.4 | async-start | bytes 5242880 | tf_op jit(solution)/shard_map/all_gather | solution.py:180
  49.7 14.3 %copy-start.11 = (bf16[1536]{0:T(1024)(128)(2,1)S(1)}, bf16[1536]{0:T(1024)(128)(2,1)}, u32[]{:S(2)}) copy-start(bf16[1536]{0:T(1024)(128)(2,1)} %param.23) | copy-start | bytes 9220
  61.7 13.2 %collective-permute-start = (bf16[4,2,64,4096]{3,2,1,0:T(8,128)(2,1)}, bf16[4,2,64,4096]{3,2,1,0:T(8,128)(2,1)}, u32[]{:S(2)}, u32[]{:S(2)}) collective-permute-start(bf16[4,2,64,4096]{3,2,1,0:T(8,128)(2,1)} %all-gather.7.cloned.1.call-done), channel_id=1, source_target_pairs={{0,1},{1,0},{2,3},{3,2},{4,5},{5,4},{6,7},{7,6},{8,9},{9,8},{10,11... | collective-permute-start | bytes 12582920 | tf_op jit(solution)/shard_map/ppermute | solution.py:186
  63.9 122.9 %reduce-scatter.5.cloned.1.call-start = ((), (), s32[]{:S(2)}) async-start(), calls=%async_computation.6 | async-start | bytes 5242880 | tf_op jit(solution)/shard_map/reduce_scatter | solution.py:183
  120.0 12.1 %copy-start.13 = (bf16[512,4096]{1,0:T(8,128)(2,1)S(1)}, bf16[512,4096]{1,0:T(8,128)(2,1)}, u32[]{:S(2)}) copy-start(bf16[512,4096]{1,0:T(8,128)(2,1)} %param.24) | copy-start | bytes 12582916
  124.7 7.4 %collective-permute-start.1 = (bf16[4,2,64,4096]{3,2,1,0:T(8,128)(2,1)S(1)}, bf16[4,2,64,4096]{3,2,1,0:T(8,128)(2,1)S(1)}, u32[]{:S(2)}, u32[]{:S(2)}) collective-permute-start(bf16[4,2,64,4096]{3,2,1,0:T(8,128)(2,1)S(1)} %convolution_convert_fusion.1), channel_id=1, source_target_pairs={{0,1},{1,0},{2,3},{3,2},{4,5},{5,4},{6,7},{7,6},{8,9},{9,8},{10,11... | collective-permute-start | bytes 12582920 | tf_op jit(solution)/shard_map/ppermute | solution.py:186
  136.4 11.9 %collective-permute-start.2 = (bf16[4,2,64,4096]{3,2,1,0:T(8,128)(2,1)}, bf16[4,2,64,4096]{3,2,1,0:T(8,128)(2,1)}, u32[]{:S(2)}, u32[]{:S(2)}) collective-permute-start(bf16[4,2,64,4096]{3,2,1,0:T(8,128)(2,1)} %all-gather.5.cloned.1.call-done), channel_id=1, source_target_pairs={{0,1},{1,0},{2,3},{3,2},{4,5},{5,4},{6,7},{7,6},{8,9},{9,8},{10,11... | collective-permute-start | bytes 12582920 | tf_op jit(solution)/shard_map/ppermute | solution.py:186
  136.9 106.5 %all-gather.11.cloned.1.call-start = ((), (), s32[]{:S(2)}) async-start(), calls=%async_computation.9 | async-start | bytes 5242880 | tf_op jit(solution)/shard_map/all_gather | solution.py:180
  186.8 4.6 copy-start.5
  188.6 1.0 copy-start.1
  191.2 103.6 %reduce-scatter.7.cloned.1.call-start = ((), (), s32[]{:S(2)}) async-start(), calls=%async_computation.7 | async-start | bytes 5242880 | tf_op jit(solution)/shard_map/reduce_scatter | solution.py:183
  192.3 51.1 %copy-start.6 = (bf16[2,4,1,64,512]{4,3,2,1,0:T(8,128)(2,1)S(1)}, bf16[2,4,1,64,512]{4,3,2,1,0:T(8,128)(2,1)}, u32[]{:S(2)}) copy-start(bf16[2,4,1,64,512]{4,3,2,1,0:T(8,128)(2,1)} %get-tuple-element.49) | copy-start | bytes 1572868
  198.9 44.6 %collective-permute-start.3 = (bf16[4,2,64,4096]{3,2,1,0:T(8,128)(2,1)}, bf16[4,2,64,4096]{3,2,1,0:T(8,128)(2,1)}, u32[]{:S(2)}, u32[]{:S(2)}) collective-permute-start(bf16[4,2,64,4096]{3,2,1,0:T(8,128)(2,1)} %convolution_convert_fusion), channel_id=1, source_target_pairs={{0,1},{1,0},{2,3},{3,2},{4,5},{5,4},{6,7},{7,6},{8,9},{9,8},{10,11... | collective-permute-start | bytes 12582920 | tf_op jit(solution)/shard_map/ppermute | solution.py:186
  243.5 8.5 %collective-permute-start.4 = (bf16[4,2,64,4096]{3,2,1,0:T(8,128)(2,1)}, bf16[4,2,64,4096]{3,2,1,0:T(8,128)(2,1)}, u32[]{:S(2)}, u32[]{:S(2)}) collective-permute-start(bf16[4,2,64,4096]{3,2,1,0:T(8,128)(2,1)} %all-gather.11.cloned.1.call-done), channel_id=1, source_target_pairs={{0,1},{1,0},{2,3},{3,2},{4,5},{5,4},{6,7},{7,6},{8,9},{9,8},{10,11... | collective-permute-start | bytes 12582920 | tf_op jit(solution)/shard_map/ppermute | solution.py:186
  251.3 91.5 %all-gather.9.cloned.1.call-start = ((), (), s32[]{:S(2)}) async-start(), calls=%async_computation.8 | async-start | bytes 5242880 | tf_op jit(solution)/shard_map/all_gather | solution.py:180
  283.1 16.1 %collective-permute-start.5 = (bf16[4,2,64,4096]{3,2,1,0:T(8,128)(2,1)}, bf16[4,2,64,4096]{3,2,1,0:T(8,128)(2,1)}, u32[]{:S(2)}, u32[]{:S(2)}) collective-permute-start(bf16[4,2,64,4096]{3,2,1,0:T(8,128)(2,1)} %fusion.24), channel_id=1, source_target_pairs={{0,1},{1,0},{2,3},{3,2},{4,5},{5,4},{6,7},{7,6},{8,9},{9,8},{10,11... | collective-permute-start | bytes 12582920 | tf_op jit(solution)/shard_map/ppermute | solution.py:186
  299.0 125.9 %reduce-scatter.11.cloned.1.call-start = ((), (), s32[]{:S(2)}) async-start(), calls=%async_computation.11 | async-start | bytes 5242880 | tf_op jit(solution)/shard_map/reduce_scatter | solution.py:183
  342.8 7.1 %collective-permute-start.6 = (bf16[4,2,64,4096]{3,2,1,0:T(8,128)(2,1)}, bf16[4,2,64,4096]{3,2,1,0:T(8,128)(2,1)}, u32[]{:S(2)}, u32[]{:S(2)}) collective-permute-start(bf16[4,2,64,4096]{3,2,1,0:T(8,128)(2,1)} %all-gather.9.cloned.1.call-done), channel_id=1, source_target_pairs={{0,1},{1,0},{2,3},{3,2},{4,5},{5,4},{6,7},{7,6},{8,9},{9,8},{10,11... | collective-permute-start | bytes 12582920 | tf_op jit(solution)/shard_map/ppermute | solution.py:186
  381.3 7.1 %collective-permute-start.7 = (bf16[4,2,64,4096]{3,2,1,0:T(8,128)(2,1)}, bf16[4,2,64,4096]{3,2,1,0:T(8,128)(2,1)}, u32[]{:S(2)}, u32[]{:S(2)}) collective-permute-start(bf16[4,2,64,4096]{3,2,1,0:T(8,128)(2,1)} %fusion.27), channel_id=1, source_target_pairs={{0,1},{1,0},{2,3},{3,2},{4,5},{5,4},{6,7},{7,6},{8,9},{9,8},{10,11... | collective-permute-start | bytes 12582920 | tf_op jit(solution)/shard_map/ppermute | solution.py:186
  381.5 88.1 %reduce-scatter.9.cloned.1.call-start = ((), (), s32[]{:S(2)}) async-start(), calls=%async_computation.10 | async-start | bytes 5242880 | tf_op jit(solution)/shard_map/reduce_scatter | solution.py:183
  420.5 4.4 copy-start.2
  420.5 49.2 %copy-start.4 = (bf16[1,2,64,4096]{3,2,1,0:T(8,128)(2,1)S(1)}, bf16[1,2,64,4096]{3,2,1,0:T(8,128)(2,1)}, u32[]{:S(2)}) copy-start(bf16[1,2,64,4096]{3,2,1,0:T(8,128)(2,1)} %copy-done.3) | copy-start | bytes 3145732
  (6 other events, 4.5 us)
Sparse Core Ops, SparseCore 0:
  14.9 46.8 all-gather.6
  64.0 44.4 all-gather.4
  137.0 45.0 reduce-scatter.4
  191.3 52.1 all-gather.10
  251.4 43.2 reduce-scatter.6
  299.1 43.6 all-gather.8
  381.7 43.1 reduce-scatter.10
  427.2 42.4 reduce-scatter.8
